TPU v7x, 128 devices: a whole 4x4x4 slice. The times are simulated.
128 devices in a mesh: section: 8 (over y, core), rep: 2 (over z_hi), tp: 8 (over z_lo, x).
Axes of the slice: x: 4, y: 4, z: 4 (z_hi: 2, z_lo: 2; z = z_hi * 2 + z_lo), core: 2. Of those that a mesh axis runs over, the one named last changes fastest.
Arguments:
- token_ids: int32 [2, 8, 128], P('rep', None, 'tp'), may hold values from 0 to 16383
- embed: bfloat16 [16384, 1024], P('section'), may hold values from -6 to 6
- w_in: bfloat16 [2, 8, 2, 1024, 2816], P('rep', 'section', None, None, 'tp'), may hold values from -0.1875 to 0.1875
- w_down: bfloat16 [2, 8, 2816, 1024], P('rep', 'section', 'tp'), may hold values from -0.109375 to 0.109375
- outer_in: float32 [8, 2, 1024, 2816], P('section', None, None, 'tp'), may hold values from -0.1875 to 0.1875
- outer_down: float32 [8, 2816, 1024], P('section', 'tp'), may hold values from -0.109375 to 0.109375
- moment_in: float32 [8, 2, 1024, 2816], P('section', None, None, 'tp'), may hold values from -0.12 to 0.12
- moment_down: float32 [8, 2816, 1024], P('section', 'tp'), may hold values from -0.12 to 0.12
- cotangent: bfloat16 [2, 8, 128, 1024], P('rep', None, 'tp'), may hold values from -6 to 6
- fragment: int32 [8], replicated, may hold values 0 or 1
Outputs:
- new_in: bfloat16 [2, 8, 2, 1024, 2816], P('rep', 'section', None, None, 'tp')
- new_down: bfloat16 [2, 8, 2816, 1024], P('rep', 'section', 'tp')
- next_outer_in: float32 [8, 2, 1024, 2816], P('section', None, None, 'tp')
- next_outer_down: float32 [8, 2816, 1024], P('section', 'tp')
- next_moment_in: float32 [8, 2, 1024, 2816], P('section', None, None, 'tp')
- next_moment_down: float32 [8, 2816, 1024], P('section', 'tp')
All inputs are finite; a program needn't handle non-finite values.
Results may differ from a plain program's by a relative error of at most 0.03.
Values may be sent and summed in bfloat16 or wider, within the bound.
A program may use at most 128 MiB of HBM per device.

v0:
```python
import jax
import jax.numpy as jnp
from jax import lax
from jax.sharding import PartitionSpec as P

EPS = 1e-05
INNER_LR = 0.001
OUTER_LR = 0.7
MOMENTUM = 0.9


def from_everyone(x, axis):
    count = lax.axis_size(axis)
    return lax.all_to_all(jnp.broadcast_to(x[None], (count, *x.shape)), axis, 0, 0, tiled=True)


def in_order(parts, dim):
    parts = jnp.moveaxis(parts, 0, dim)
    dims = parts.shape
    return parts.reshape(*dims[:dim], dims[dim] * dims[dim + 1], *dims[dim + 2 :])


def collect(x, axis, dim):
    parts = from_everyone(x, axis)
    return in_order(parts, dim)


def from_behind(value, axis, steps):
    count = lax.axis_size(axis)
    initial, last = (max(0, -steps), min(count, count - steps))
    return lax.ppermute(value, axis, [(source, source + steps) for source in range(initial, last)])


def cut_along(x, dim, count):
    before, after = (x.shape[:dim], x.shape[dim + 1 :])
    return jnp.moveaxis(x.reshape(*before, count, -1, *after), dim, 0)


def sum_at_owner(x, axis, dim):
    parts = cut_along(x, dim, lax.axis_size(axis))
    arrived = lax.all_to_all(parts, axis, split_axis=0, concat_axis=0, tiled=True)
    return arrived.astype(jnp.float32).sum(axis=0)


def scale_rows(values):
    return lax.rsqrt(jnp.mean(values * values, axis=-1, keepdims=True) + EPS)


def gather_rows(values):
    return collect(values, "tp", 0)


def pass_along(values, step):
    return from_behind(values, "section", step)


def reduce_rows(left, right, form):
    return sum_at_owner(
        jnp.einsum(form, left, right, preferred_element_type=jnp.float32).astype(jnp.bfloat16),
        "tp",
        0,
    )


def layer_forward(x_own, pair, down):
    full = gather_rows(x_own).astype(jnp.float32)
    normed = (full * scale_rows(full)).astype(jnp.bfloat16)
    gate_up = jnp.einsum("td,kdf->tkf", normed, pair, preferred_element_type=jnp.float32)
    hidden = (jax.nn.silu(gate_up[:, 0]) * gate_up[:, 1]).astype(jnp.bfloat16)
    out = reduce_rows(hidden, down, "tf,fd->td")
    return ((x_own.astype(jnp.float32) + out).astype(jnp.bfloat16), normed, gate_up)


def layer_backward(grad_own, x_own, pair, down, normed, gate_up):
    grad_full = gather_rows(grad_own)
    d_hidden = jnp.einsum("td,fd->tf", grad_full, down, preferred_element_type=jnp.float32)
    gate = gate_up[:, 0]
    upper = gate_up[:, 1]
    sig = jax.nn.sigmoid(gate)
    active = jax.nn.silu(gate)
    hidden = (active * upper).astype(jnp.bfloat16)
    d_both = jnp.stack(
        [d_hidden * upper * sig * (1.0 + gate * (1.0 - sig)), d_hidden * active], axis=1
    ).astype(jnp.bfloat16)
    g_down = jnp.einsum("tf,td->fd", hidden, grad_full, preferred_element_type=jnp.float32)
    g_pair = jnp.einsum("td,tkf->kdf", normed, d_both, preferred_element_type=jnp.float32)
    d_norm = reduce_rows(d_both, pair, "tkf,kdf->td")
    xf = x_own.astype(jnp.float32)
    rinv = scale_rows(xf)
    d_x = (
        grad_own.astype(jnp.float32)
        + rinv * d_norm
        - xf * (rinv * rinv * rinv) * jnp.mean(d_norm * xf, axis=-1, keepdims=True)
    )
    return (d_x.astype(jnp.bfloat16), g_pair, g_down)


def shards(
    token_ids,
    embed,
    w_in,
    w_down,
    outer_in,
    outer_down,
    moment_in,
    moment_down,
    cotangent,
    fragment,
):
    sections = lax.axis_size("section")
    section = lax.axis_index("section")
    replicas = lax.axis_size("rep")
    ids = token_ids[0]
    batches, own_rows = ids.shape
    vocab_part, width = embed.shape
    local_ids = ids - section * vocab_part
    inside = (local_ids >= 0) & (local_ids < vocab_part)
    looked = jnp.take(embed, jnp.clip(local_ids, 0, vocab_part - 1), axis=0).astype(jnp.float32)
    looked = jnp.where(inside[:, :, None], looked, 0.0)
    start_rows = lax.psum(looked.astype(jnp.bfloat16), "section")
    pairs = w_in[0]
    downs = w_down[0]
    depth = pairs.shape[0]
    hidden_width = pairs.shape[-1]
    total_rows = own_rows * lax.axis_size("tp")
    ticks = batches + sections - 1
    first = section == 0
    final = section == sections - 1

    def forward_tick(tick, carry):
        inbox, x_store, normed_store, gate_store = carry
        micro = tick - section
        valid = (micro >= 0) & (micro < batches)
        slot = jnp.where(valid, micro, batches)
        feed = lax.dynamic_index_in_dim(
            start_rows, jnp.clip(tick, 0, batches - 1).astype(jnp.int32), 0, keepdims=False
        )
        current = jnp.where(first, feed, inbox)
        zero = jnp.zeros((), jnp.int32)
        x_store = lax.dynamic_update_slice(
            x_store, current[None, None], (slot, zero + 0, zero, zero)
        )
        current, normed, gate_up = layer_forward(current, pairs[0], downs[0])
        normed_store = lax.dynamic_update_slice(
            normed_store, normed[None, None], (slot, zero + 0, zero, zero)
        )
        gate_store = lax.dynamic_update_slice(
            gate_store, gate_up[None, None], (slot, zero + 0, zero, zero, zero)
        )
        return (pass_along(current, 1), x_store, normed_store, gate_store)

    start_carry = (
        jnp.zeros((own_rows, width), jnp.bfloat16),
        jnp.zeros((batches + 1, depth, own_rows, width), jnp.bfloat16),
        jnp.zeros((batches + 1, depth, total_rows, width), jnp.bfloat16),
        jnp.zeros((batches + 1, depth, total_rows, 2, hidden_width), jnp.float32),
    )
    _, x_store, normed_store, gate_store = lax.fori_loop(0, ticks, forward_tick, start_carry)
    seeds = cotangent[0]

    def backward_tick(tick, carry):
        inbox, acc_pair, acc_down = carry
        micro = tick - (sections - 1 - section)
        valid = (micro >= 0) & (micro < batches)
        index = jnp.clip(micro, 0, batches - 1)
        feed = lax.dynamic_index_in_dim(seeds, index, 0, keepdims=False)
        grad = jnp.where(final, feed, inbox)
        grad = jnp.where(valid, grad, jnp.zeros_like(grad))
        zero = jnp.zeros((), jnp.int32)
        for layer in reversed(range(depth)):
            x_own = lax.dynamic_slice(
                x_store, (index, zero + layer, zero, zero), (1, 1, own_rows, width)
            )[0, 0]
            normed = lax.dynamic_slice(
                normed_store, (index, zero + layer, zero, zero), (1, 1, total_rows, width)
            )[0, 0]
            gate_up = lax.dynamic_slice(
                gate_store,
                (index, zero + layer, zero, zero, zero),
                (1, 1, total_rows, 2, hidden_width),
            )[0, 0]
            grad, g_pair, g_down = layer_backward(
                grad, x_own, pairs[layer], downs[layer], normed, gate_up
            )
            acc_pair = acc_pair.at[layer].add(g_pair)
            acc_down = acc_down.at[layer].add(g_down)
        return (pass_along(grad, -1), acc_pair, acc_down)

    back_carry = (
        jnp.zeros((own_rows, width), jnp.bfloat16),
        jnp.zeros(pairs.shape, jnp.float32),
        jnp.zeros(downs.shape, jnp.float32),
    )
    _, acc_pair, acc_down = lax.fori_loop(0, ticks, backward_tick, back_carry)
    new_pair = (pairs.astype(jnp.float32) - INNER_LR * acc_pair).astype(jnp.bfloat16)
    new_out = (downs.astype(jnp.float32) - INNER_LR * acc_down).astype(jnp.bfloat16)
    every_pair, every_down = (
        lax.all_gather(new_pair[None], "rep", axis=0, tiled=True),
        lax.all_gather(new_out[None], "rep", axis=0, tiled=True),
    )
    sum_pair = jnp.sum(every_pair.astype(jnp.float32), axis=0)
    sum_down = jnp.sum(every_down.astype(jnp.float32), axis=0)
    mean_pair = outer_in - sum_pair / replicas
    mean_down = outer_down - sum_down / replicas
    flag = lax.dynamic_index_in_dim(fragment, section, 0, keepdims=False)
    chosen = flag == 1
    moment_pair = MOMENTUM * moment_in + mean_pair
    moment_out = MOMENTUM * moment_down + mean_down
    outer_pair = outer_in - OUTER_LR * (mean_pair + MOMENTUM * moment_pair)
    outer_out = outer_down - OUTER_LR * (mean_down + MOMENTUM * moment_out)
    result_pair = jnp.where(chosen, outer_pair.astype(jnp.bfloat16), new_pair)
    result_down = jnp.where(chosen, outer_out.astype(jnp.bfloat16), new_out)
    return (
        result_pair[None],
        result_down[None],
        jnp.where(chosen, outer_pair, outer_in),
        jnp.where(chosen, outer_out, outer_down),
        jnp.where(chosen, moment_pair, moment_in),
        jnp.where(chosen, moment_out, moment_down),
    )


def solution(mesh):
    return jax.shard_map(
        shards,
        mesh=mesh,
        in_specs=(
            P("rep", None, "tp"),
            P("section", None),
            P("rep", "section", None, None, "tp"),
            P("rep", "section", "tp", None),
            P("section", None, None, "tp"),
            P("section", "tp", None),
            P("section", None, None, "tp"),
            P("section", "tp", None),
            P("rep", None, "tp", None),
            P(),
        ),
        out_specs=(
            P("rep", "section", None, None, "tp"),
            P("rep", "section", "tp", None),
            P("section", None, None, "tp"),
            P("section", "tp", None),
            P("section", None, None, "tp"),
            P("section", "tp", None),
        ),
        check_vma=False,
    )
```

profile of v0, /device:TPU:0, one launch (start us, length us, event | category | flops | bytes accessed | tf_op | source)
XLA Modules:
  0.0 1122.3 jit_solution(13803856848150441553)
XLA Ops:
  14.1 62.9 %all-reduce.2.cloned.1.call-done = bf16[8,16,1024]{2,1,0:T(8,128)(2,1)} async-done(((bf16[8,16,1024]{2,1,0:T(8,128)(2,1)}), bf16[8,16,1024]{2,1,0:T(8,128)(2,1)}) %all-reduce.2.cloned.1.call-update) | async-done | bytes 262160 | tf_op jit(solution)/shard_map/psum | solution.py:120
  81.6 442.3 %while.42 = (s32[]{:T(128)}, bf16[16,1024]{1,0:T(8,128)(2,1)S(1)}, bf16[9,1,16,1024]{3,2,1,0:T(8,128)(2,1)}, bf16[9,1,128,1024]{3,2,1,0:T(8,128)(2,1)}, f32[9,1,...) while((s32[]{:T(128)}, bf16[16,1024]{1,0:T(8,128)(2,1)S(1)}, ...), condition=%wide.region_4.5_spmd, body=%wide.region_1.4_spmd.sunk | while | flops 278716544 | bytes 10293609 | solution.py:158
  83.1 12.3 %all_to_all.50 = bf16[8,16,1024]{2,1,0:T(8,128)(2,1)S(1)} all-to-all(bf16[8,16,1024]{2,1,0:T(8,128)(2,1)S(1)} %broadcast_in_dim.132), channel_id=1, replica_groups=mesh['section'=8,'rep'=2,'tp'=8] {'tp'}, dimensions={0} | all-to-all | bytes 524288 | tf_op jit(solution)/shard_map/while/body/eval_jaxpr/all_to_all | solution.py:14
  112.3 10.5 all_to_all.50
  128.9 7.3 all-to-all-done.1
  139.9 10.0 all_to_all.50
  155.9 8.5 all-to-all-done.1
  168.8 9.8 all_to_all.50
  184.8 8.2 all-to-all-done.1
  197.4 9.8 all_to_all.50
  226.9 9.8 all_to_all.50
  242.9 7.2 all-to-all-done.1
  256.8 9.8 all_to_all.50
  272.7 7.2 all-to-all-done.1
  286.6 9.8 all_to_all.50
  316.4 9.8 all_to_all.50
  332.4 7.2 all-to-all-done.1
  346.3 9.8 all_to_all.50
  362.2 7.2 all-to-all-done.1
  376.1 9.8 all_to_all.50
  392.1 7.2 all-to-all-done.1
  406.0 9.8 all_to_all.50
  421.9 7.2 all-to-all-done.1
  435.8 9.8 all_to_all.50
  451.7 7.2 all-to-all-done.1
  465.7 9.8 all_to_all.50
  481.6 7.2 all-to-all-done.1
  495.5 9.8 all_to_all.50
  511.4 7.2 all-to-all-done.1
  524.5 495.4 %while.43 = (s32[]{:T(128)}, bf16[16,1024]{1,0:T(8,128)(2,1)}, f32[1,2,1024,352]{2,3,1,0:T(8,128)}, f32[1,352,1024]{2,1,0:T(8,128)S(1)}, s32[]{:T(128)}, /*index...) while((s32[]{:T(128)}, bf16[16,1024]{1,0:T(8,128)(2,1)}, ...), condition=%wide.region_9.10_spmd.clone, body=%wide.region_5.9_spmd.clone.sunk | while | flops 557469760 | bytes 18695212 | solution.py:194
  1027.0 32.0 %all-gather.7.cloned.1.call-done = bf16[2,352,1024]{2,1,0:T(8,128)(2,1)} async-done(((bf16[1,352,1024]{2,1,0:T(8,128)(2,1)}), bf16[2,352,1024]{2,1,0:T(8,128)(2,1)}) %all-gather.7.cloned.1.call-update) | async-done | bytes 1441808 | tf_op jit(solution)/shard_map/all_gather | solution.py:199
  1064.5 42.0 %all-gather.5.cloned.1.call-done = bf16[2,2,1024,352]{2,3,1,0:T(8,128)(2,1)} async-done(((bf16[1,2,1024,352]{2,3,1,0:T(8,128)(2,1)}), bf16[2,2,1024,352]{2,3,1,0:T(8,128)(2,1)}) %all-gather.5.cloned.1.call-update) | async-done | bytes 2883600 | tf_op jit(solution)/shard_map/all_gather | solution.py:198
  (633 shorter events, 729.3 us)
Async XLA Ops:
  7.2 69.9 %all-reduce.2.cloned.1.call-start = ((), (), s32[]{:S(2)}) async-start(), calls=%async_computation.4 | async-start | bytes 524288 | tf_op jit(solution)/shard_map/psum | solution.py:120
  14.1 1044.9 %all-gather.7.cloned.1.call-start = ((), (), s32[]{:S(2)}) async-start(), calls=%async_computation.6 | async-start | bytes 2162688 | tf_op jit(solution)/shard_map/all_gather | solution.py:199
  125.4 10.8 all-to-all-start.1
  152.4 12.0 %all-to-all-start.1 = ((bf16[8,16,1024]{2,1,0:T(8,128)(2,1)}), bf16[8,16,1024]{2,1,0:T(8,128)(2,1)S(1)}, u32[]{:S(2)}, u32[]{:S(2)}) async-start(bf16[8,16,1024]{2,1,0:T(8,128)(2,1)} %bitcast.213), calls=%async_computation.1 | async-start | bytes 524288 | tf_op jit(solution)/shard_map/while/body/eval_jaxpr/all_to_all | solution.py:41
  181.3 11.7 %all-to-all-start.1 = ((bf16[8,16,1024]{2,1,0:T(8,128)(2,1)}), bf16[8,16,1024]{2,1,0:T(8,128)(2,1)S(1)}, u32[]{:S(2)}, u32[]{:S(2)}) async-start(bf16[8,16,1024]{2,1,0:T(8,128)(2,1)} %bitcast.213), calls=%async_computation.1 | async-start | bytes 524288 | tf_op jit(solution)/shard_map/while/body/eval_jaxpr/all_to_all | solution.py:41
  239.4 10.7 all-to-all-start.1
  269.2 10.7 all-to-all-start.1
  299.1 10.7 all-to-all-start.1
  328.9 10.7 all-to-all-start.1
  358.7 10.7 all-to-all-start.1
  388.6 10.7 all-to-all-start.1
  418.4 10.7 all-to-all-start.1
  448.2 10.7 all-to-all-start.1
  478.1 10.7 all-to-all-start.1
  507.9 10.7 all-to-all-start.1
  539.8 10.7 all-to-all-start.3
  592.8 10.7 all-to-all-start.2
  606.7 10.7 all-to-all-start.3
  625.8 10.7 all-to-all-start.2
  639.7 10.7 all-to-all-start.3
  672.6 10.7 all-to-all-start.3
  705.6 10.7 all-to-all-start.3
  738.6 10.7 all-to-all-start.3
  771.5 10.7 all-to-all-start.3
  804.5 10.7 all-to-all-start.3
  837.5 10.7 all-to-all-start.3
  870.5 10.7 all-to-all-start.3
  903.4 10.7 all-to-all-start.3
  936.4 10.7 all-to-all-start.3
  969.4 10.7 all-to-all-start.3
  1002.3 10.7 all-to-all-start.3
  1022.1 84.4 %all-gather.5.cloned.1.call-start = ((), (), s32[]{:S(2)}) async-start(), calls=%async_computation.5 | async-start | bytes 4325376 | tf_op jit(solution)/shard_map/all_gather | solution.py:198
  (114 other events, 882.2 us)
Sparse Core Ops, SparseCore 0:
  14.2 62.8 all-reduce.1
  1022.3 36.6 all-gather.6
  1061.2 45.3 all-gather.4
where the time goes:
time: 1130 us; the launch traced here: 1120 us
  waiting for transfers between devices  425 us (38%)
  starting transfers between devices  227 us (20%)
  matrix products  157 us (14%)
  blocking collectives  150 us (13%)
  other arithmetic  100 us (9%)
  local copies, waits for them, and re-layouts  46.6 us (4%)
  between operations  14.6 us (1%)
    all_to_all x30, waiting for transfers between devices, sum_at_owner(): lax.all_to_all(parts, axis, split_axis=0, concat_axis=0, tiled=True)  159 us
    all_to_all x15, blocking collectives, from_everyone(): lax.all_to_all(jnp.broadcast_to(x[None], (count, *x.shape)), axis, 0, 0,...  150 us
    all_to_all x30, starting transfers between devices, sum_at_owner(): lax.all_to_all(parts, axis, split_axis=0, concat_axis=0, tiled=True)  102 us
    all_to_all x15, waiting for transfers between devices, from_everyone(): lax.all_to_all(jnp.broadcast_to(x[None], (count, *x.shape)), axis, 0, 0,...  93.2 us
    ppermute x30, starting transfers between devices, from_behind(): lax.ppermute(value, axis, [(source, source + steps) for source in range(i...  73 us
    psum x1, waiting for transfers between devices, shards(): start_rows = lax.psum(looked.astype(jnp.bfloat16), 'section')  62.9 us
    dot_general x15, matrix products, layer_backward(): jnp.einsum('td,tkf->kdf', normed, d_both, preferred_element_type=jnp.floa...  60.7 us
    all_to_all x15, starting transfers between devices, from_everyone(): lax.all_to_all(jnp.broadcast_to(x[None], (count, *x.shape)), axis, 0, 0,...  51.2 us
  transfers between devices with their start and end apart: 78, of which 63 were waited for; matrix products, arithmetic and copies ran while one was open for 11% of the time, Pallas kernels for 0%

commit v1 on v0

v1 whole, which is shorter than its diff:
```python
import functools

import jax
import jax.numpy as jnp
from jax import lax
from jax.experimental import pallas as pl
from jax.experimental.pallas import tpu as pltpu
from jax.sharding import PartitionSpec as P

EPS = 1e-05
INNER_LR = 0.001
OUTER_LR = 0.7
MOMENTUM = 0.9
MESH = pl.DeviceIdType.MESH
BF16 = jnp.bfloat16
F32 = jnp.float32
NT = (((1,), (1,)), ((), ()))
TN = (((0,), (0,)), ((), ()))


def relay_kernel(
    S, N, ZX,
    looked, cot, w_gate, w_up, w_down,
    new_gate, new_up, new_down,
    ag_f, rs_f, res_f, out_f, x_own, x_next,
    ag_b, rs_b, res_b, out_b,
    gate_s, up_s, hid_s, dg_s, du_s,
    ag_f_in, rs_f_in, res_f_in, x_next_in, ag_b_in, rs_b_in, res_b_in,
    ag_f_out, rs_f_out, res_f_out, x_next_out, ag_b_out, rs_b_out, res_b_out, emb_out,
):
    s = lax.axis_index("section")
    t = lax.axis_index("tp")
    M, _, R, D = ag_f.shape
    T = N * R
    first, final = s == 0, s == S - 1
    X = ZX
    tz, tx = t // X, lax.rem(t, X)
    hops = [(dz, dx) for dz in range(N // X) for dx in range(X) if (dz, dx) != (0, 0)]
    hops.sort(key=lambda h: -(h[0] + min(h[1], X - h[1])))
    peers = [lax.rem(tz + dz, N // X) * X + lax.rem(tx + dx, X) for dz, dx in hops]
    up_s_id = jnp.minimum(s + 1, S - 1)
    down_s_id = jnp.maximum(s - 1, 0)

    def send(src, dst, out, arrive, section, tp):
        pltpu.make_async_remote_copy(
            src_ref=src, dst_ref=dst, send_sem=out, recv_sem=arrive,
            device_id={"section": section, "tp": tp}, device_id_type=MESH,
        ).start()

    def drain(ref, sem):
        pltpu.make_async_copy(ref, ref, sem).wait()

    barrier = pltpu.get_barrier_semaphore()

    def greet(section, tp):
        pl.semaphore_signal(
            barrier, inc=1, device_id={"section": section, "tp": tp}, device_id_type=MESH
        )

    for peer in peers:
        greet(s, peer)

    @pl.when(jnp.logical_not(final))
    def _():
        for k in range(N):
            greet(up_s_id, lax.rem(t + k, N))

    @pl.when(jnp.logical_not(first))
    def _():
        for k in range(N):
            greet(down_s_id, lax.rem(t + k, N))

    @pl.when(first)
    def _():
        for other in range(2, S):
            greet(other, t)
        pl.semaphore_wait(barrier, N - 1 + N + S - 2)

    @pl.when(s == 1)
    def _():
        pl.semaphore_wait(barrier, N - 1 + 2 * N)

    @pl.when(s > 1)
    def _():
        greet(0, t)

        @pl.when(final)
        def _():
            pl.semaphore_wait(barrier, N - 1 + N + 1)

        @pl.when(jnp.logical_not(final))
        def _():
            pl.semaphore_wait(barrier, N - 1 + 2 * N + 1)

    @pl.when(jnp.logical_not(first))
    def _():
        @pl.loop(0, M)
        def _(m):
            send(looked.at[m], rs_f.at[m, s], emb_out, rs_f_in.at[m], 0, t)

    def gather_grad(m):
        for peer in peers:
            send(ag_b.at[m, t], ag_b.at[m, t], ag_b_out.at[m], ag_b_in.at[m], s, peer)

        @pl.when(jnp.logical_not(first))
        def _():
            send(ag_b.at[m, t], res_b.at[m], res_b_out.at[m], res_b_in.at[m], down_s_id, t)

    @pl.when(final)
    def _():
        @pl.loop(0, M)
        def _(m):
            ag_b[m, t] = cot[m]
            gather_grad(m)

    def rinv_of(x):
        return lax.rsqrt(jnp.mean(x * x, axis=-1, keepdims=True) + EPS)

    def forward_own(m):
        @pl.when(first)
        def _():
            drain(rs_f.at[m, pl.ds(1, S - 1)], rs_f_in.at[m])
            total = looked[m].astype(F32)
            for j in range(1, S):
                total = total + rs_f[m, j].astype(F32)
            x_own[m] = total.astype(BF16)

        @pl.when(jnp.logical_not(first))
        def _():
            drain(rs_f.at[m], rs_f_in.at[m])
            drain(res_f.at[m], res_f_in.at[m])
            total = rs_f[m, 0].astype(F32)
            for j in range(1, N):
                total = total + rs_f[m, j].astype(F32)
            x_own[m] = (res_f[m].astype(F32) + total).astype(BF16)

        x = x_own[m].astype(F32)
        ag_f[m, t] = (x * rinv_of(x)).astype(BF16)
        for peer in peers:
            send(ag_f.at[m, t], ag_f.at[m, t], ag_f_out.at[m], ag_f_in.at[m], s, peer)

        @pl.when(jnp.logical_not(final))
        def _():
            send(x_own.at[m], res_f.at[m], res_f_out.at[m], res_f_in.at[m], up_s_id, t)

        @pl.when(jnp.logical_not(first))
        def _():
            send(x_own.at[m], x_next.at[m], x_next_out.at[m], x_next_in.at[m], down_s_id, t)

    def forward_all(m):
        drain(ag_f.at[m, pl.ds(0, N - 1)], ag_f_in.at[m])
        normed = ag_f[m].reshape(T, D)
        gate = jnp.dot(normed, w_gate[...], preferred_element_type=F32)
        upper = jnp.dot(normed, w_up[...], preferred_element_type=F32)
        hidden = (jax.nn.silu(gate) * upper).astype(BF16)
        gate_s[m] = gate
        up_s[m] = upper
        hid_s[m] = hidden

        @pl.when(jnp.logical_not(final))
        def _():
            part = jnp.dot(hidden, w_down[...], preferred_element_type=F32)
            out_f[m] = part.astype(BF16).reshape(N, R, D)
            for k in range(N):
                to = lax.rem(t + k, N)
                send(out_f.at[m, to], rs_f.at[m, t], rs_f_out.at[m], rs_f_in.at[m], up_s_id, to)

    @pl.loop(0, M + 1)
    def _(step):
        @pl.when(step < M)
        def _():
            forward_own(step)

        @pl.when(step > 0)
        def _():
            forward_all(step - 1)

    def backward_own(m):
        drain(rs_b.at[m], rs_b_in.at[m])
        drain(res_b.at[m], res_b_in.at[m])
        drain(x_next.at[m], x_next_in.at[m])
        d_norm = rs_b[m, 0].astype(F32)
        for j in range(1, N):
            d_norm = d_norm + rs_b[m, j].astype(F32)
        x = x_next[m].astype(F32)
        rinv = rinv_of(x)
        d_x = (
            res_b[m].astype(F32)
            + rinv * d_norm
            - x * (rinv * rinv * rinv) * jnp.mean(d_norm * x, axis=-1, keepdims=True)
        )
        ag_b[m, t] = d_x.astype(BF16)
        gather_grad(m)

    def backward_all(m):
        drain(ag_b.at[m, pl.ds(0, N - 1)], ag_b_in.at[m])
        grad = ag_b[m].reshape(T, D)
        d_hidden = lax.dot_general(grad, w_down[...], NT, preferred_element_type=F32)
        gate = gate_s[m]
        upper = up_s[m]
        sig = jax.nn.sigmoid(gate)
        d_gate = (d_hidden * upper * sig * (1.0 + gate * (1.0 - sig))).astype(BF16)
        d_up = (d_hidden * (gate * sig)).astype(BF16)
        dg_s[m] = d_gate
        du_s[m] = d_up

        @pl.when(jnp.logical_not(first))
        def _():
            part = lax.dot_general(d_gate, w_gate[...], NT, preferred_element_type=F32)
            part = part + lax.dot_general(d_up, w_up[...], NT, preferred_element_type=F32)
            out_b[m] = part.astype(BF16).reshape(N, R, D)
            for k in range(N):
                to = lax.rem(t + k, N)
                send(out_b.at[m, to], rs_b.at[m, t], rs_b_out.at[m], rs_b_in.at[m], down_s_id, to)

    @pl.loop(0, M + 1)
    def _(step):
        @pl.when((step < M) & jnp.logical_not(final))
        def _():
            backward_own(step)

        @pl.when(step > 0)
        def _():
            backward_all(step - 1)

    H = dg_s.shape[-1]
    wide = 256

    @pl.loop(0, D // wide)
    def _(c):
        cols = pl.ds(pl.multiple_of(c * wide, wide), wide)
        normed = ag_f[:, :, :, cols].reshape(M * T, wide)
        g = lax.dot_general(normed, dg_s[...].reshape(M * T, H), TN, preferred_element_type=F32)
        new_gate[cols, :] = (w_gate[cols, :].astype(F32) - INNER_LR * g).astype(BF16)
        g = lax.dot_general(normed, du_s[...].reshape(M * T, H), TN, preferred_element_type=F32)
        new_up[cols, :] = (w_up[cols, :].astype(F32) - INNER_LR * g).astype(BF16)
        grad = ag_b[:, :, :, cols].reshape(M * T, wide)
        g = lax.dot_general(hid_s[...].reshape(M * T, H), grad, TN, preferred_element_type=F32)
        new_down[:, cols] = (w_down[:, cols].astype(F32) - INNER_LR * g).astype(BF16)

    @pl.when(jnp.logical_not(first))
    def _():
        drain(looked, emb_out)

    @pl.when(final)
    def _():
        @pl.loop(0, M)
        def _(m):
            drain(x_next.at[m], x_next_out.at[m])
            drain(out_b.at[m], rs_b_out.at[m])
            drain(res_b.at[m], res_b_out.at[m])

    @pl.when(first)
    def _():
        @pl.loop(0, M)
        def _(m):
            drain(res_f.at[m], res_f_out.at[m])
            drain(out_f.at[m], rs_f_out.at[m])

    @pl.when(jnp.logical_not(first | final))
    def _():
        @pl.loop(0, M)
        def _(m):
            drain(res_f.at[m], res_f_out.at[m])
            drain(out_f.at[m], rs_f_out.at[m])
            drain(x_next.at[m], x_next_out.at[m])
            drain(out_b.at[m], rs_b_out.at[m])
            drain(res_b.at[m], res_b_out.at[m])

    @pl.loop(0, M)
    def _(m):
        drain(ag_f.at[m, pl.ds(0, N - 1)], ag_f_out.at[m])
        drain(ag_b.at[m, pl.ds(0, N - 1)], ag_b_out.at[m])


def relay(looked, cot, pair, down):
    S, N = lax.axis_size("section"), lax.axis_size("tp")
    M, R, D = looked.shape
    H = down.shape[0]
    T = N * R
    vm = pltpu.VMEM
    dma = pltpu.SemaphoreType.DMA((M,))
    scratch = [
        vm((M, N, R, D), BF16), vm((M, N, R, D), BF16), vm((M, R, D), BF16),
        vm((M, N, R, D), BF16), vm((M, R, D), BF16), vm((M, R, D), BF16),
        vm((M, N, R, D), BF16), vm((M, N, R, D), BF16), vm((M, R, D), BF16),
        vm((M, N, R, D), BF16),
        vm((M, T, H), F32), vm((M, T, H), F32),
        vm((M, T, H), BF16), vm((M, T, H), BF16), vm((M, T, H), BF16),
    ] + [dma] * 14 + [pltpu.SemaphoreType.DMA]
    spec = pl.BlockSpec(memory_space=pltpu.VMEM)
    return pl.pallas_call(
        functools.partial(relay_kernel, S, N, 4 if N % 4 == 0 else N),
        out_shape=(
            jax.ShapeDtypeStruct((D, H), BF16),
            jax.ShapeDtypeStruct((D, H), BF16),
            jax.ShapeDtypeStruct((H, D), BF16),
        ),
        in_specs=[spec] * 5,
        out_specs=[spec] * 3,
        scratch_shapes=scratch,
        compiler_params=pltpu.CompilerParams(
            collective_id=0, has_side_effects=True, vmem_limit_bytes=56 * 1024 * 1024
        ),
        name="relay",
    )(looked, cot, pair[0], pair[1], down)


def shards(
    token_ids,
    embed,
    w_in,
    w_down,
    outer_in,
    outer_down,
    moment_in,
    moment_down,
    cotangent,
    fragment,
):
    section = lax.axis_index("section")
    replicas = lax.axis_size("rep")
    ids = token_ids[0]
    vocab_part, width = embed.shape
    local_ids = ids - section * vocab_part
    inside = (local_ids >= 0) & (local_ids < vocab_part)
    looked = jnp.take(embed, jnp.clip(local_ids, 0, vocab_part - 1), axis=0)
    looked = jnp.where(inside[:, :, None], looked, jnp.zeros_like(looked))
    pair = w_in[0, 0]
    down = w_down[0, 0]
    new_gate, new_up, new_out = relay(looked, cotangent[0], pair, down)
    new_pair = jnp.stack([new_gate, new_up])
    swap = [(r, (r + 1) % replicas) for r in range(replicas)]
    other_pair = lax.ppermute(new_pair, "rep", swap)
    other_out = lax.ppermute(new_out, "rep", swap)
    mean_pair = outer_in[0] - (new_pair.astype(F32) + other_pair.astype(F32)) / replicas
    mean_down = outer_down[0] - (new_out.astype(F32) + other_out.astype(F32)) / replicas
    flag = lax.dynamic_index_in_dim(fragment, section, 0, keepdims=False)
    chosen = flag == 1
    moment_pair = MOMENTUM * moment_in[0] + mean_pair
    moment_out = MOMENTUM * moment_down[0] + mean_down
    outer_pair = outer_in[0] - OUTER_LR * (mean_pair + MOMENTUM * moment_pair)
    outer_out = outer_down[0] - OUTER_LR * (mean_down + MOMENTUM * moment_out)
    result_pair = jnp.where(chosen, outer_pair.astype(BF16), new_pair)
    result_down = jnp.where(chosen, outer_out.astype(BF16), new_out)
    return (
        result_pair[None, None],
        result_down[None, None],
        jnp.where(chosen, outer_pair, outer_in[0])[None],
        jnp.where(chosen, outer_out, outer_down[0])[None],
        jnp.where(chosen, moment_pair, moment_in[0])[None],
        jnp.where(chosen, moment_out, moment_down[0])[None],
    )


def solution(mesh):
    return jax.shard_map(
        shards,
        mesh=mesh,
        in_specs=(
            P("rep", None, "tp"),
            P("section", None),
            P("rep", "section", None, None, "tp"),
            P("rep", "section", "tp", None),
            P("section", None, None, "tp"),
            P("section", "tp", None),
            P("section", None, None, "tp"),
            P("section", "tp", None),
            P("rep", None, "tp", None),
            P(),
        ),
        out_specs=(
            P("rep", "section", None, None, "tp"),
            P("rep", "section", "tp", None),
            P("section", None, None, "tp"),
            P("section", "tp", None),
            P("section", None, None, "tp"),
            P("section", "tp", None),
        ),
        check_vma=False,
    )
```

time: 1130 us -> 392 us (0.35)
  waiting for transfers between devices: 425 us -> 20.3 us
  Pallas kernels: 0 us -> 317 us
  starting transfers between devices: 227 us -> 5.09 us
  matrix products: 157 us -> 0 us
  blocking collectives: 150 us -> 0 us
  other arithmetic: 100 us -> 21.6 us
  local copies, waits for them, and re-layouts: 46.6 us -> 26.5 us
  between operations: 14.6 us -> 1.36 us
    pallas_call x0 -> x1, Pallas kernels: none -> 317 us  [relay(): pl.pallas_call(functools.partial(relay_kernel, S, N, 4 if N % 4 == 0 else...]
    all_to_all x45 -> x0, waiting for transfers between devices: 252 us -> none  [the longest x30 159 us: sum_at_owner(): lax.all_to_all(parts, axis, split_axis=0, concat_axis=0, tiled=True)]
    dot_general x90 -> x0, matrix products: 157 us -> none  [the longest x15 60.7 us: layer_backward(): jnp.einsum('td,tkf->kdf', normed, d_both, preferred_element_type=jnp.floa...]
    all_to_all x45 -> x0, starting transfers between devices: 154 us -> none  [the longest x30 102 us: sum_at_owner(): lax.all_to_all(parts, axis, split_axis=0, concat_axis=0, tiled=True)]
    all_to_all x15 -> x0, blocking collectives: 150 us -> none  [from_everyone(): lax.all_to_all(jnp.broadcast_to(x[None], (count, *x.shape)), axis, 0, 0,...]
    all_gather x2 -> x0, waiting for transfers between devices: 74 us -> none  [the longest x1 42 us: shards(): lax.all_gather(new_pair[None], 'rep', axis=0, tiled=True)]
    ppermute x30 -> x2, starting transfers between devices: 73 us -> 5.09 us  [the longest x1 5.07 us: shards(): other_out = lax.ppermute(new_out, 'rep', swap)]
    psum x1 -> x0, waiting for transfers between devices: 62.9 us -> none  [shards(): start_rows = lax.psum(looked.astype(jnp.bfloat16), 'section')]
  transfers between devices with their start and end apart: 78 -> 2, of which waited for: 63 -> 2; matrix products, arithmetic and copies ran while one was open for 11% -> 4% of each run, Pallas kernels for 0% -> 0%
where the time goes in v1:
time: 392 us; the launch traced here: 391 us
  Pallas kernels  317 us (81%)
  local copies, waits for them, and re-layouts  26.5 us (7%)
  other arithmetic  21.6 us (6%)
  waiting for transfers between devices  20.3 us (5%)
  starting transfers between devices  5.09 us (1%)
    pallas_call x1, Pallas kernels, relay(): pl.pallas_call(functools.partial(relay_kernel, S, N, 4 if N % 4 == 0 else...  317 us
    unnamed x25, local copies, waits for them, and re-layouts  16.5 us
    ppermute x1, waiting for transfers between devices, shards(): other_pair = lax.ppermute(new_pair, 'rep', swap)  13.3 us
  transfers between devices with their start and end apart: 2, of which 2 were waited for; matrix products, arithmetic and copies ran while one was open for 4% of the time, Pallas kernels for 0%

profile of v1, /device:TPU:0, one launch (start us, length us, event | category | flops | bytes accessed | tf_op | source)
XLA Modules:
  0.0 391.4 jit_solution(14990329485145716969)
XLA Ops:
  0.6 0.7 compare_select_fusion
  1.3 0.7 compare_and_fusion
  2.0 0.7 and_bitcast_fusion
  2.7 0.1 reshape.69
  2.8 1.4 fusion.6
  4.2 1.2 copy.32
  5.4 1.2 copy.33
  6.6 3.8 gather_fusion
  10.3 0.8 select_select_fusion.looked
  11.1 316.6 %relay.1 = (bf16[1024,352]{1,0:T(8,128)(2,1)}, bf16[1024,352]{1,0:T(8,128)(2,1)}, bf16[352,1024]{1,0:T(8,128)(2,1)}) custom-call(bf16[8,16,1024]{2,1,0:T(8,128)(2,1)} %select_select_fusion.looked, bf16[8,16,1024]{2,1,0:T(8,128)(2,1)} %bitcast.98, bf16[1024,352]{1,0:T(8,128)(2,1)} %bitcast.94, bf16[1024,352]{1,0:T(8,128)(2,1)} %bitcast.95, ...), custom_call_target="tpu_custom_call" | custom-call | tf_op jit(solution)/shard_map/relay/pallas_call | solution.py:292
  327.8 5.1 %collective-permute-start.1 = (bf16[352,1024]{1,0:T(8,128)(2,1)}, bf16[352,1024]{1,0:T(8,128)(2,1)}, u32[]{:S(2)}, u32[]{:S(2)}) collective-permute-start(bf16[352,1024]{1,0:T(8,128)(2,1)} %get-tuple-element.11), channel_id=1, source_target_pairs={{0,8},{8,0},{1,9},{9,1},{2,10},{10,2},{3,11},{11,3},{4,12},{12,4},... | collective-permute-start | bytes 2162696 | tf_op jit(solution)/shard_map/ppermute | solution.py:335
  332.9 1.7 pad_maximum_fusion
  334.5 1.6 copy.26
  336.1 0.0 collective-permute-start
  336.1 2.3 copy.28
  338.5 0.0 copy-start.8
  338.5 3.5 copy.23
  342.0 0.0 copy-done.8
  342.0 0.6 dynamic_slice.4
  343.2 7.0 %collective-permute-done.1 = bf16[352,1024]{1,0:T(8,128)(2,1)} collective-permute-done((bf16[352,1024]{1,0:T(8,128)(2,1)}, bf16[352,1024]{1,0:T(8,128)(2,1)}, u32[]{:S(2)}, u32[]{:S(2)}) %collective-permute-start.1) | collective-permute-done | bytes 720928 | tf_op jit(solution)/shard_map/ppermute | solution.py:335
  350.2 4.2 %select_bitcast_fusion.1 = bf16[1,1,352,1024]{3,2,1,0:T(8,128)(2,1)} fusion(bf16[352,1024]{1,0:T(8,128)(2,1)} %get-tuple-element.11, pred[]{:T(512)} %bitcast, f32[1,352,1024]{2,1,0:T(8,128)} %param.17, bf16[352,1024]{1,0:T(8,128)(2,1)} %collective-permute-done.1, f32[1,352,1024]{2,1,0:T(8,128)} %param.15), kind=kLoop, calls=%fused_computation.19 | loop fusion | flops 4685824 | bytes 5046273 | tf_op jit(solution)/shard_map/broadcast_in_dim | solution.py:348
  354.3 0.0 copy-done.5
  354.3 0.0 copy-done.6
  354.3 0.0 copy-done.7
  354.3 3.3 fusion.4
  357.7 13.3 %collective-permute-done = bf16[2,1024,352]{1,2,0:T(8,128)(2,1)} collective-permute-done((bf16[2,1024,352]{1,2,0:T(8,128)(2,1)}, bf16[2,1024,352]{1,2,0:T(8,128)(2,1)}, u32[]{:S(2)}, u32[]{:S(2)}) %collective-permute-start) | collective-permute-done | bytes 1441824 | tf_op jit(solution)/shard_map/ppermute | solution.py:334
  371.0 2.6 copy.27
  373.5 5.5 %select_bitcast_fusion = bf16[1,1,2,1024,352]{4,3,2,1,0:T(8,128)(2,1)} fusion(pred[]{:T(512)} %bitcast, f32[1,2,1024,352]{3,2,1,0:T(8,128)S(1)} %copy.28, bf16[2,1024,352]{2,1,0:T(8,128)(2,1)} %copy.27, f32[1,2,1024,352]{3,2,1,0:T(8,128)} %copy.23, bf16[1,1024,352]{2,1,0:T(8,128)(2,1)} %bitcast.92, bf16[1,1024,352]{2,1,0:T(8,128)(2,1)} %bitcast.89), kind=kLoop, calls=%fused_computation.10 | loop fusion | flops 10092544 | bytes 10092545 | tf_op jit(solution)/shard_map/broadcast_in_dim | solution.py:347
  379.1 4.0 %fusion.1 = (f32[1,2,1024,352]{3,2,1,0:T(8,128)}, f32[1,2,1024,352]{3,2,1,0:T(8,128)}) fusion(f32[1,2,1024,352]{3,2,1,0:T(8,128)S(1)} %copy.28, bf16[2,1024,352]{2,1,0:T(8,128)(2,1)S(1)} %copy-done.1, f32[1,2,1024,352]{3,2,1,0:T(8,128)S(1)} %copy-done, pred[]{:T(512)} %bitcast, bf16[1,1024,352]{2,1,0:T(8,128)(2,1)S(1)} %bitcast.93, ...), kind=kLoop, calls=%fused_computation.4 | loop fusion | flops 10092544 | bytes 14417921 | tf_op jit(solution)/shard_map/broadcast_in_dim | solution.py:351
  383.1 2.5 copy.29
  385.6 3.6 copy.30
  389.2 2.3 copy.31
  (14 shorter events, 0.0 us)
Async XLA Ops:
  327.8 22.4 %collective-permute-start.1 = (bf16[352,1024]{1,0:T(8,128)(2,1)}, bf16[352,1024]{1,0:T(8,128)(2,1)}, u32[]{:S(2)}, u32[]{:S(2)}) collective-permute-start(bf16[352,1024]{1,0:T(8,128)(2,1)} %get-tuple-element.11), channel_id=1, source_target_pairs={{0,8},{8,0},{1,9},{9,1},{2,10},{10,2},{3,11},{11,3},{4,12},{12,4},... | collective-permute-start | bytes 2162696 | tf_op jit(solution)/shard_map/ppermute | solution.py:335
  336.1 34.9 %collective-permute-start = (bf16[2,1024,352]{1,2,0:T(8,128)(2,1)}, bf16[2,1024,352]{1,2,0:T(8,128)(2,1)}, u32[]{:S(2)}, u32[]{:S(2)}) collective-permute-start(bf16[2,1024,352]{1,2,0:T(8,128)(2,1)} %copy.26), channel_id=1, source_target_pairs={{0,8},{8,0},{1,9},{9,1},{2,10},{10,2},{3,11},{11,3},{4,12},{12,4},... | collective-permute-start | bytes 4325384 | tf_op jit(solution)/shard_map/ppermute | solution.py:334
  338.5 3.5 copy-start.8
  350.2 4.2 %copy-start.5 = (f32[1,352,1024]{2,1,0:T(8,128)S(1)}, f32[1,352,1024]{2,1,0:T(8,128)}, u32[]{:S(2)}) copy-start(f32[1,352,1024]{2,1,0:T(8,128)} %param.17) | copy-start | bytes 4325380
  350.2 4.2 %copy-start.6 = (f32[1,352,1024]{2,1,0:T(8,128)S(1)}, f32[1,352,1024]{2,1,0:T(8,128)}, u32[]{:S(2)}) copy-start(f32[1,352,1024]{2,1,0:T(8,128)} %param.15) | copy-start | bytes 4325380
  350.2 4.2 %copy-start.7 = (bf16[352,1024]{1,0:T(8,128)(2,1)S(1)}, bf16[352,1024]{1,0:T(8,128)(2,1)}, u32[]{:S(2)}) copy-start(bf16[352,1024]{1,0:T(8,128)(2,1)} %get-tuple-element.11) | copy-start | bytes 2162692
  373.5 5.5 %copy-start = (f32[1,2,1024,352]{3,2,1,0:T(8,128)S(1)}, f32[1,2,1024,352]{3,2,1,0:T(8,128)}, u32[]{:S(2)}) copy-start(f32[1,2,1024,352]{3,2,1,0:T(8,128)} %copy.23) | copy-start | bytes 8650756
  373.5 5.5 %copy-start.1 = (bf16[2,1024,352]{2,1,0:T(8,128)(2,1)S(1)}, bf16[2,1024,352]{2,1,0:T(8,128)(2,1)}, u32[]{:S(2)}) copy-start(bf16[2,1024,352]{2,1,0:T(8,128)(2,1)} %copy.27) | copy-start | bytes 4325380
  373.5 5.5 %copy-start.3 = (bf16[1024,352]{1,0:T(8,128)(2,1)S(1)}, bf16[1024,352]{1,0:T(8,128)(2,1)}, u32[]{:S(2)}) copy-start(bf16[1024,352]{1,0:T(8,128)(2,1)} %get-tuple-element.9) | copy-start | bytes 2162692
  373.5 5.5 %copy-start.4 = (bf16[1024,352]{1,0:T(8,128)(2,1)S(1)}, bf16[1024,352]{1,0:T(8,128)(2,1)}, u32[]{:S(2)}) copy-start(bf16[1024,352]{1,0:T(8,128)(2,1)} %get-tuple-element.10) | copy-start | bytes 2162692
  385.6 3.6 copy-start.2

commit v2 on v1

--- a/solution.py
+++ b/solution.py
@@ -20,7 +20,7 @@
 
 def relay_kernel(
     S, N, ZX,
-    looked, cot, w_gate, w_up, w_down,
+    looked, cot, w_in, w_down,
     new_gate, new_up, new_down,
     ag_f, rs_f, res_f, out_f, x_own, x_next,
     ag_b, rs_b, res_b, out_b,
@@ -150,8 +150,8 @@
     def forward_all(m):
         drain(ag_f.at[m, pl.ds(0, N - 1)], ag_f_in.at[m])
         normed = ag_f[m].reshape(T, D)
-        gate = jnp.dot(normed, w_gate[...], preferred_element_type=F32)
-        upper = jnp.dot(normed, w_up[...], preferred_element_type=F32)
+        gate = lax.dot_general(normed, w_in[0], NT, preferred_element_type=F32)
+        upper = lax.dot_general(normed, w_in[1], NT, preferred_element_type=F32)
         hidden = (jax.nn.silu(gate) * upper).astype(BF16)
         gate_s[m] = gate
         up_s[m] = upper
@@ -161,19 +161,20 @@
         def _():
             part = jnp.dot(hidden, w_down[...], preferred_element_type=F32)
             out_f[m] = part.astype(BF16).reshape(N, R, D)
-            for k in range(N):
-                to = lax.rem(t + k, N)
+            for to in peers + [t]:
                 send(out_f.at[m, to], rs_f.at[m, t], rs_f_out.at[m], rs_f_in.at[m], up_s_id, to)
 
-    @pl.loop(0, M + 1)
+    @pl.loop(0, M + 2)
     def _(step):
-        @pl.when(step < M)
-        def _():
-            forward_own(step)
-
-        @pl.when(step > 0)
-        def _():
-            forward_all(step - 1)
+        own = step - jnp.where(first, 0, 1)
+
+        @pl.when((own >= 0) & (own < M))
+        def _():
+            forward_own(own)
+
+        @pl.when(step > 1)
+        def _():
+            forward_all(step - 2)
 
     def backward_own(m):
         drain(rs_b.at[m], rs_b_in.at[m])
@@ -206,11 +207,10 @@
 
         @pl.when(jnp.logical_not(first))
         def _():
-            part = lax.dot_general(d_gate, w_gate[...], NT, preferred_element_type=F32)
-            part = part + lax.dot_general(d_up, w_up[...], NT, preferred_element_type=F32)
+            part = jnp.dot(d_gate, w_in[0], preferred_element_type=F32)
+            part = part + jnp.dot(d_up, w_in[1], preferred_element_type=F32)
             out_b[m] = part.astype(BF16).reshape(N, R, D)
-            for k in range(N):
-                to = lax.rem(t + k, N)
+            for to in peers + [t]:
                 send(out_b.at[m, to], rs_b.at[m, t], rs_b_out.at[m], rs_b_in.at[m], down_s_id, to)
 
     @pl.loop(0, M + 1)
@@ -230,10 +230,10 @@
     def _(c):
         cols = pl.ds(pl.multiple_of(c * wide, wide), wide)
         normed = ag_f[:, :, :, cols].reshape(M * T, wide)
-        g = lax.dot_general(normed, dg_s[...].reshape(M * T, H), TN, preferred_element_type=F32)
-        new_gate[cols, :] = (w_gate[cols, :].astype(F32) - INNER_LR * g).astype(BF16)
-        g = lax.dot_general(normed, du_s[...].reshape(M * T, H), TN, preferred_element_type=F32)
-        new_up[cols, :] = (w_up[cols, :].astype(F32) - INNER_LR * g).astype(BF16)
+        g = lax.dot_general(dg_s[...].reshape(M * T, H), normed, TN, preferred_element_type=F32)
+        new_gate[:, cols] = (w_in[0, :, cols].astype(F32) - INNER_LR * g).astype(BF16)
+        g = lax.dot_general(du_s[...].reshape(M * T, H), normed, TN, preferred_element_type=F32)
+        new_up[:, cols] = (w_in[1, :, cols].astype(F32) - INNER_LR * g).astype(BF16)
         grad = ag_b[:, :, :, cols].reshape(M * T, wide)
         g = lax.dot_general(hid_s[...].reshape(M * T, H), grad, TN, preferred_element_type=F32)
         new_down[:, cols] = (w_down[:, cols].astype(F32) - INNER_LR * g).astype(BF16)
@@ -292,18 +292,55 @@
     return pl.pallas_call(
         functools.partial(relay_kernel, S, N, 4 if N % 4 == 0 else N),
         out_shape=(
-            jax.ShapeDtypeStruct((D, H), BF16),
-            jax.ShapeDtypeStruct((D, H), BF16),
             jax.ShapeDtypeStruct((H, D), BF16),
-        ),
-        in_specs=[spec] * 5,
+            jax.ShapeDtypeStruct((H, D), BF16),
+            jax.ShapeDtypeStruct((H, D), BF16),
+        ),
+        in_specs=[spec] * 4,
         out_specs=[spec] * 3,
         scratch_shapes=scratch,
         compiler_params=pltpu.CompilerParams(
             collective_id=0, has_side_effects=True, vmem_limit_bytes=56 * 1024 * 1024
         ),
         name="relay",
-    )(looked, cot, pair[0], pair[1], down)
+    )(looked, cot, pair, down)
+
+
+def outer_kernel(flag, inner, other, outer, moment, *rest):
+    new, next_outer, next_moment = rest[-3:]
+    chosen = flag[0] == 1
+    own = inner[...].astype(F32)
+    before = outer[0]
+    mean = before - (own + other[...].astype(F32)) / 2
+    moved = MOMENTUM * moment[0] + mean
+    after = before - OUTER_LR * (mean + MOMENTUM * moved)
+    new[0] = jnp.where(chosen, after, own).astype(BF16)
+    next_outer[0] = jnp.where(chosen, after, before)
+    next_moment[0] = jnp.where(chosen, moved, moment[0])
+
+
+def outer_step(flag, inner, other, outer, moment, part, earlier=()):
+    H, D = inner.shape
+    rows, wide = H // 2, D // 2
+    small = pl.BlockSpec((rows, wide), lambda i, j: (i, j))
+    block = pl.BlockSpec((1, rows, wide), lambda i, j: (part, i, j))
+    return pl.pallas_call(
+        outer_kernel,
+        grid=(H // rows, D // wide),
+        out_shape=(
+            jax.ShapeDtypeStruct(outer.shape, BF16),
+            jax.ShapeDtypeStruct(outer.shape, F32),
+            jax.ShapeDtypeStruct(outer.shape, F32),
+        ),
+        in_specs=[pl.BlockSpec(memory_space=pltpu.SMEM), small, small, block, block]
+        + [pl.BlockSpec(memory_space=pl.ANY)] * len(earlier),
+        out_specs=(block, block, block),
+        input_output_aliases={5 + i: i for i in range(len(earlier))},
+        cost_estimate=pl.CostEstimate(
+            flops=10 * H * D, bytes_accessed=22 * H * D, transcendentals=0
+        ),
+        name="outer_step",
+    )(flag, inner, other, outer, moment, *earlier)
 
 
 def shards(
@@ -326,30 +363,31 @@
     inside = (local_ids >= 0) & (local_ids < vocab_part)
     looked = jnp.take(embed, jnp.clip(local_ids, 0, vocab_part - 1), axis=0)
     looked = jnp.where(inside[:, :, None], looked, jnp.zeros_like(looked))
-    pair = w_in[0, 0]
-    down = w_down[0, 0]
-    new_gate, new_up, new_out = relay(looked, cotangent[0], pair, down)
-    new_pair = jnp.stack([new_gate, new_up])
+    rows = 8
+    looked = looked.reshape(-1, rows, width)
+    seeds = cotangent.reshape(-1, rows, width)
+    pair = jnp.swapaxes(w_in[0, 0], 1, 2)
+    new_gate, new_up, new_out = relay(looked, seeds, pair, w_down[0, 0])
     swap = [(r, (r + 1) % replicas) for r in range(replicas)]
-    other_pair = lax.ppermute(new_pair, "rep", swap)
-    other_out = lax.ppermute(new_out, "rep", swap)
-    mean_pair = outer_in[0] - (new_pair.astype(F32) + other_pair.astype(F32)) / replicas
-    mean_down = outer_down[0] - (new_out.astype(F32) + other_out.astype(F32)) / replicas
-    flag = lax.dynamic_index_in_dim(fragment, section, 0, keepdims=False)
-    chosen = flag == 1
-    moment_pair = MOMENTUM * moment_in[0] + mean_pair
-    moment_out = MOMENTUM * moment_down[0] + mean_down
-    outer_pair = outer_in[0] - OUTER_LR * (mean_pair + MOMENTUM * moment_pair)
-    outer_out = outer_down[0] - OUTER_LR * (mean_down + MOMENTUM * moment_out)
-    result_pair = jnp.where(chosen, outer_pair.astype(BF16), new_pair)
-    result_down = jnp.where(chosen, outer_out.astype(BF16), new_out)
+    flag = lax.dynamic_slice(fragment, (section,), (1,))
+    outer_pair = jnp.swapaxes(outer_in[0], 1, 2)
+    moment_pair = jnp.swapaxes(moment_in[0], 1, 2)
+    done = outer_step(flag, new_gate, lax.ppermute(new_gate, "rep", swap), outer_pair, moment_pair, 0)
+    done = outer_step(
+        flag, new_up, lax.ppermute(new_up, "rep", swap), outer_pair, moment_pair, 1, done
+    )
+    last = outer_step(
+        flag, new_out, lax.ppermute(new_out, "rep", swap), outer_down, moment_down, 0
+    )
+    pair_new, pair_outer, pair_moment = (jnp.swapaxes(part, 1, 2) for part in done)
+    down_new, down_outer, down_moment = last
     return (
-        result_pair[None, None],
-        result_down[None, None],
-        jnp.where(chosen, outer_pair, outer_in[0])[None],
-        jnp.where(chosen, outer_out, outer_down[0])[None],
-        jnp.where(chosen, moment_pair, moment_in[0])[None],
-        jnp.where(chosen, moment_out, moment_down[0])[None],
+        pair_new[None, None],
+        down_new[None],
+        pair_outer[None],
+        down_outer,
+        pair_moment[None],
+        down_moment,
     )
 
 

time: 392 us -> 308 us (0.79)
  Pallas kernels: 317 us -> 267 us
  other arithmetic: 21.6 us -> 2.22 us
  local copies, waits for them, and re-layouts: 26.5 us -> 7.17 us
    pallas_call x1, Pallas kernels: 317 us -> 251 us  [relay(): pl.pallas_call(functools.partial(relay_kernel, S, N, 4 if N % 4 == 0 else...]
    broadcast_in_dim x4 -> x0, other arithmetic: 17 us -> none  [the longest x1 5.5 us: shards(): result_pair[None, None]]
    pallas_call x0 -> x3, Pallas kernels: none -> 16 us  [outer_step(): pl.pallas_call(outer_kernel, grid=(H // rows, D // wide), out_shape=(jax....]
    unnamed x25 -> x8, local copies, waits for them, and re-layouts: 16.5 us -> 2.6 us
    ppermute x2 -> x3, waiting for transfers between devices: 20.3 us -> 22.9 us  [the longest x1 13.1 us: shards(): lax.ppermute(new_gate, 'rep', swap)]
  transfers between devices with their start and end apart: 2 -> 3, of which waited for: 2 -> 3; matrix products, arithmetic and copies ran while one was open for 4% -> 0% of each run, Pallas kernels for 0% -> 3%
where the time goes in v2:
time: 308 us; the launch traced here: 307 us
  Pallas kernels  267 us (87%)
  waiting for transfers between devices  22.9 us (7%)
  starting transfers between devices  7.63 us (2%)
  local copies, waits for them, and re-layouts  7.17 us (2%)
    pallas_call x1, Pallas kernels, relay(): pl.pallas_call(functools.partial(relay_kernel, S, N, 4 if N % 4 == 0 else...  251 us
    pallas_call x3, Pallas kernels, outer_step(): pl.pallas_call(outer_kernel, grid=(H // rows, D // wide), out_shape=(jax....  16 us
    ppermute x1, waiting for transfers between devices, shards(): lax.ppermute(new_gate, 'rep', swap)  13.1 us
    ppermute x1, waiting for transfers between devices, shards(): lax.ppermute(new_out, 'rep', swap)  8.35 us
  transfers between devices with their start and end apart: 3, of which 3 were waited for; matrix products, arithmetic and copies ran while one was open for 0% of the time, Pallas kernels for 3%

profile of v2, /device:TPU:0, one launch (start us, length us, event | category | flops | bytes accessed | tf_op | source)
XLA Modules:
  0.0 307.3 jit_solution(8917392472634742752)
XLA Ops:
  0.6 0.0 copy-start.3
  0.6 0.7 compare_select_fusion.1
  1.3 0.7 compare_and_fusion.1
  2.0 0.1 reshape.73
  2.1 0.1 min.16
  2.2 0.1 and.20
  2.3 3.8 %gather_fusion = bf16[128,1024]{1,0:T(8,128)(2,1)S(1)} fusion(bf16[2048,1024]{1,0:T(8,128)(2,1)} %param.11, s32[1024]{0:T(1024)S(1)} %pad_clamp_fusion), kind=kCustom, calls=%fused_computation | custom fusion | bytes 524800 | tf_op jit(solution)/shard_map/jit(_take)/gather | solution.py:364
  6.1 0.8 fusion.looked
  6.9 250.6 %relay.1 = (bf16[352,1024]{1,0:T(8,128)(2,1)}, bf16[352,1024]{1,0:T(8,128)(2,1)}, bf16[352,1024]{1,0:T(8,128)(2,1)}) custom-call(bf16[16,8,1024]{2,1,0:T(8,128)(2,1)} %fusion.looked, bf16[16,8,1024]{2,1,0:T(8,128)(2,1)} %bitcast.38, bf16[2,352,1024]{2,1,0:T(8,128)(2,1)} %bitcast.35, bf16[352,1024]{1,0:T(8,128)(2,1)} %bitcast.37), custom_call_target="tpu_custom_call" | custom-call | tf_op jit(solution)/shard_map/relay/pallas_call | solution.py:292
  257.5 4.1 %collective-permute-start.1 = (bf16[352,1024]{1,0:T(8,128)(2,1)}, bf16[352,1024]{1,0:T(8,128)(2,1)S(1)}, u32[]{:S(2)}, u32[]{:S(2)}) collective-permute-start(bf16[352,1024]{1,0:T(8,128)(2,1)} %get-tuple-element.19.inner), channel_id=1, source_target_pairs={{0,8},{8,0},{1,9},{9,1},{2,10},{10,2},{3,11},{11,3},{4,12},{12,4},... | collective-permute-start | bytes 2162696 | tf_op jit(solution)/shard_map/ppermute | solution.py:375
  261.6 0.1 collective-permute-start.2
  261.7 3.4 %collective-permute-start = (bf16[352,1024]{1,0:T(8,128)(2,1)}, bf16[352,1024]{1,0:T(8,128)(2,1)S(1)}, u32[]{:S(2)}, u32[]{:S(2)}) collective-permute-start(bf16[352,1024]{1,0:T(8,128)(2,1)} %get-tuple-element.18.inner), channel_id=1, source_target_pairs={{0,8},{8,0},{1,9},{9,1},{2,10},{10,2},{3,11},{11,3},{4,12},{12,4},... | collective-permute-start | bytes 2162696 | tf_op jit(solution)/shard_map/ppermute | solution.py:377
  265.1 0.0 copy-done.3
  265.1 0.6 dynamic_slice.3.flag
  265.7 13.1 %collective-permute-done.1.other = bf16[352,1024]{1,0:T(8,128)(2,1)S(1)} collective-permute-done((bf16[352,1024]{1,0:T(8,128)(2,1)}, bf16[352,1024]{1,0:T(8,128)(2,1)S(1)}, u32[]{:S(2)}, u32[]{:S(2)}) %collective-permute-start.1) | collective-permute-done | bytes 720928 | tf_op jit(solution)/shard_map/ppermute | solution.py:375
  278.8 0.0 copy-start.1
  278.8 0.9 copy-done.1
  279.6 5.3 %outer_step.3 = (bf16[2,352,1024]{2,1,0:T(8,128)(2,1)}, f32[2,352,1024]{2,1,0:T(8,128)}, f32[2,352,1024]{2,1,0:T(8,128)}) custom-call(s32[1]{0:T(128)} %dynamic_slice.3.flag, bf16[352,1024]{1,0:T(8,128)(2,1)} %get-tuple-element.19.inner, bf16[352,1024]{1,0:T(8,128)(2,1)} %copy-done.1, f32[2,352,1024]{2,1,0:T(8,128)} %bitcast.29, f32[2,352,1024]{2,1,0:T(8,128)} %bitcast.31), custom_call_target="tpu_custom_call" | custom-call | flops 3604480 | bytes 7929856 | tf_op jit(solution)/shard_map/outer_step/pallas_call | solution.py:327
  285.0 8.3 %collective-permute-done.2.other = bf16[352,1024]{1,0:T(8,128)(2,1)S(1)} collective-permute-done((bf16[352,1024]{1,0:T(8,128)(2,1)}, bf16[352,1024]{1,0:T(8,128)(2,1)S(1)}, u32[]{:S(2)}, u32[]{:S(2)}) %collective-permute-start.2) | collective-permute-done | bytes 720928 | tf_op jit(solution)/shard_map/ppermute | solution.py:380
  293.3 0.0 copy-start
  293.3 0.9 copy-done
  294.2 5.3 %outer_step.5 = (bf16[1,352,1024]{2,1,0:T(8,128)(2,1)}, f32[1,352,1024]{2,1,0:T(8,128)}, f32[1,352,1024]{2,1,0:T(8,128)}) custom-call(s32[1]{0:T(128)} %dynamic_slice.3.flag, bf16[352,1024]{1,0:T(8,128)(2,1)} %get-tuple-element.24.inner, bf16[352,1024]{1,0:T(8,128)(2,1)} %copy-done, f32[1,352,1024]{2,1,0:T(8,128)} %outer.1, f32[1,352,1024]{2,1,0:T(8,128)} %moment.1), custom_call_target="tpu_custom_call" | custom-call | flops 3604480 | bytes 7929856 | tf_op jit(solution)/shard_map/outer_step/pallas_call | solution.py:327
  299.5 1.5 collective-permute-done.other
  301.1 0.0 copy-start.2
  301.1 0.9 copy-done.2
  301.9 5.3 %outer_step.4 = (bf16[2,352,1024]{2,1,0:T(8,128)(2,1)}, f32[2,352,1024]{2,1,0:T(8,128)}, f32[2,352,1024]{2,1,0:T(8,128)}) custom-call(s32[1]{0:T(128)} %dynamic_slice.3.flag, bf16[352,1024]{1,0:T(8,128)(2,1)} %get-tuple-element.18.inner, bf16[352,1024]{1,0:T(8,128)(2,1)} %copy-done.2, ...), custom_call_target="tpu_custom_call", output_to_operand_aliasing={{0}: (5, {}), {1}: (6, {}), {2}: (7, {})} | custom-call | flops 3604480 | bytes 7929856 | tf_op jit(solution)/shard_map/outer_step/pallas_call | solution.py:327
  (2 shorter events, 0.0 us)
Async XLA Ops:
  0.6 264.5 %copy-start.3 = (s32[8]{0:T(128)S(1)}, s32[8]{0:T(128)}, u32[]{:S(2)}) copy-start(s32[8]{0:T(128)} %param.19) | copy-start | bytes 100
  257.5 21.3 %collective-permute-start.1 = (bf16[352,1024]{1,0:T(8,128)(2,1)}, bf16[352,1024]{1,0:T(8,128)(2,1)S(1)}, u32[]{:S(2)}, u32[]{:S(2)}) collective-permute-start(bf16[352,1024]{1,0:T(8,128)(2,1)} %get-tuple-element.19.inner), channel_id=1, source_target_pairs={{0,8},{8,0},{1,9},{9,1},{2,10},{10,2},{3,11},{11,3},{4,12},{12,4},... | collective-permute-start | bytes 2162696 | tf_op jit(solution)/shard_map/ppermute | solution.py:375
  261.6 31.7 %collective-permute-start.2 = (bf16[352,1024]{1,0:T(8,128)(2,1)}, bf16[352,1024]{1,0:T(8,128)(2,1)S(1)}, u32[]{:S(2)}, u32[]{:S(2)}) collective-permute-start(bf16[352,1024]{1,0:T(8,128)(2,1)} %get-tuple-element.24.inner), channel_id=1, source_target_pairs={{0,8},{8,0},{1,9},{9,1},{2,10},{10,2},{3,11},{11,3},{4,12},{12,4},... | collective-permute-start | bytes 2162696 | tf_op jit(solution)/shard_map/ppermute | solution.py:380
  261.7 39.4 %collective-permute-start = (bf16[352,1024]{1,0:T(8,128)(2,1)}, bf16[352,1024]{1,0:T(8,128)(2,1)S(1)}, u32[]{:S(2)}, u32[]{:S(2)}) collective-permute-start(bf16[352,1024]{1,0:T(8,128)(2,1)} %get-tuple-element.18.inner), channel_id=1, source_target_pairs={{0,8},{8,0},{1,9},{9,1},{2,10},{10,2},{3,11},{11,3},{4,12},{12,4},... | collective-permute-start | bytes 2162696 | tf_op jit(solution)/shard_map/ppermute | solution.py:377
  278.8 0.9 copy-start.1
  293.3 0.9 copy-start
  301.1 0.9 copy-start.2

commit v3 on v2

--- a/solution.py
+++ b/solution.py
@@ -12,6 +12,8 @@
 OUTER_LR = 0.7
 MOMENTUM = 0.9
 MESH = pl.DeviceIdType.MESH
+EARLY = 3
+LAG = 6
 BF16 = jnp.bfloat16
 F32 = jnp.float32
 NT = (((1,), (1,)), ((), ()))
@@ -26,7 +28,7 @@
     ag_b, rs_b, res_b, out_b,
     gate_s, up_s, hid_s, dg_s, du_s,
     ag_f_in, rs_f_in, res_f_in, x_next_in, ag_b_in, rs_b_in, res_b_in,
-    ag_f_out, rs_f_out, res_f_out, x_next_out, ag_b_out, rs_b_out, res_b_out, emb_out,
+    ag_f_out, rs_f_out, res_f_out, x_next_out, ag_b_out, rs_b_out, res_b_out, emb_out, go,
 ):
     s = lax.axis_index("section")
     t = lax.axis_index("tp")
@@ -94,7 +96,7 @@
 
     @pl.when(jnp.logical_not(first))
     def _():
-        @pl.loop(0, M)
+        @pl.loop(0, EARLY)
         def _(m):
             send(looked.at[m], rs_f.at[m, s], emb_out, rs_f_in.at[m], 0, t)
 
@@ -163,18 +165,6 @@
             out_f[m] = part.astype(BF16).reshape(N, R, D)
             for to in peers + [t]:
                 send(out_f.at[m, to], rs_f.at[m, t], rs_f_out.at[m], rs_f_in.at[m], up_s_id, to)
-
-    @pl.loop(0, M + 2)
-    def _(step):
-        own = step - jnp.where(first, 0, 1)
-
-        @pl.when((own >= 0) & (own < M))
-        def _():
-            forward_own(own)
-
-        @pl.when(step > 1)
-        def _():
-            forward_all(step - 2)
 
     def backward_own(m):
         drain(rs_b.at[m], rs_b_in.at[m])
@@ -213,15 +203,42 @@
             for to in peers + [t]:
                 send(out_b.at[m, to], rs_b.at[m, t], rs_b_out.at[m], rs_b_in.at[m], down_s_id, to)
 
-    @pl.loop(0, M + 1)
+    @pl.when(jnp.logical_not(first))
+    def _():
+        pl.semaphore_wait(go, 1)
+
+        @pl.loop(EARLY, M)
+        def _(m):
+            send(looked.at[m], rs_f.at[m, s], emb_out, rs_f_in.at[m], 0, t)
+
+    lag = jnp.minimum(M, LAG * (S - 1 - s))
+
+    @pl.loop(0, M + 1 + lag)
     def _(step):
-        @pl.when((step < M) & jnp.logical_not(final))
-        def _():
-            backward_own(step)
-
-        @pl.when(step > 0)
-        def _():
-            backward_all(step - 1)
+        @pl.when(step < M)
+        def _():
+            forward_own(step)
+
+        @pl.when(first & (step == 0))
+        def _():
+            for other in range(1, S):
+                pl.semaphore_signal(
+                    go, inc=1, device_id={"section": other, "tp": t}, device_id_type=MESH
+                )
+
+        @pl.when((step > 0) & (step <= M))
+        def _():
+            forward_all(step - 1)
+
+        back = step - lag
+
+        @pl.when((back >= 0) & (back < M) & jnp.logical_not(final))
+        def _():
+            backward_own(back)
+
+        @pl.when((back > 0) & (back <= M))
+        def _():
+            backward_all(back - 1)
 
     H = dg_s.shape[-1]
     wide = 256
@@ -287,7 +304,7 @@
         vm((M, N, R, D), BF16),
         vm((M, T, H), F32), vm((M, T, H), F32),
         vm((M, T, H), BF16), vm((M, T, H), BF16), vm((M, T, H), BF16),
-    ] + [dma] * 14 + [pltpu.SemaphoreType.DMA]
+    ] + [dma] * 14 + [pltpu.SemaphoreType.DMA, pltpu.SemaphoreType.REGULAR]
     spec = pl.BlockSpec(memory_space=pltpu.VMEM)
     return pl.pallas_call(
         functools.partial(relay_kernel, S, N, 4 if N % 4 == 0 else N),

time: 308 us -> 276 us (0.90)
  Pallas kernels: 267 us -> 235 us
    pallas_call x1, Pallas kernels: 251 us -> 219 us  [relay(): pl.pallas_call(functools.partial(relay_kernel, S, N, 4 if N % 4 == 0 else...]
  transfers between devices with their start and end apart: 3 -> 3, of which waited for: 3 -> 3; matrix products, arithmetic and copies ran while one was open for 0% -> 0% of each run, Pallas kernels for 3% -> 4%
where the time goes in v3:
time: 276 us; the launch traced here: 275 us
  Pallas kernels  235 us (85%)
  waiting for transfers between devices  23.6 us (9%)
  local copies, waits for them, and re-layouts  7.17 us (3%)
  starting transfers between devices  6.55 us (2%)
    pallas_call x1, Pallas kernels, relay(): pl.pallas_call(functools.partial(relay_kernel, S, N, 4 if N % 4 == 0 else...  219 us
    pallas_call x3, Pallas kernels, outer_step(): pl.pallas_call(outer_kernel, grid=(H // rows, D // wide), out_shape=(jax....  16 us
    ppermute x1, waiting for transfers between devices, shards(): lax.ppermute(new_gate, 'rep', swap)  13.7 us
    ppermute x1, waiting for transfers between devices, shards(): lax.ppermute(new_out, 'rep', swap)  8.4 us
  transfers between devices with their start and end apart: 3, of which 3 were waited for; matrix products, arithmetic and copies ran while one was open for 0% of the time, Pallas kernels for 4%

profile of v3, /device:TPU:0, one launch (start us, length us, event | category | flops | bytes accessed | tf_op | source)
XLA Modules:
  0.0 275.0 jit_solution(7263665587369077986)
XLA Ops:
  0.6 0.0 copy-start.3
  0.6 0.7 compare_select_fusion.1
  1.3 0.7 compare_and_fusion.1
  2.0 0.1 reshape.73
  2.1 0.1 min.16
  2.2 0.1 and.20
  2.3 3.8 %gather_fusion = bf16[128,1024]{1,0:T(8,128)(2,1)S(1)} fusion(bf16[2048,1024]{1,0:T(8,128)(2,1)} %param.11, s32[1024]{0:T(1024)S(1)} %pad_clamp_fusion), kind=kCustom, calls=%fused_computation | custom fusion | bytes 524800 | tf_op jit(solution)/shard_map/jit(_take)/gather | solution.py:381
  6.1 0.8 fusion.looked
  6.9 218.8 %relay.1 = (bf16[352,1024]{1,0:T(8,128)(2,1)}, bf16[352,1024]{1,0:T(8,128)(2,1)}, bf16[352,1024]{1,0:T(8,128)(2,1)}) custom-call(bf16[16,8,1024]{2,1,0:T(8,128)(2,1)} %fusion.looked, bf16[16,8,1024]{2,1,0:T(8,128)(2,1)} %bitcast.38, bf16[2,352,1024]{2,1,0:T(8,128)(2,1)} %bitcast.35, bf16[352,1024]{1,0:T(8,128)(2,1)} %bitcast.37), custom_call_target="tpu_custom_call" | custom-call | tf_op jit(solution)/shard_map/relay/pallas_call | solution.py:309
  225.7 3.0 %collective-permute-start.1 = (bf16[352,1024]{1,0:T(8,128)(2,1)}, bf16[352,1024]{1,0:T(8,128)(2,1)S(1)}, u32[]{:S(2)}, u32[]{:S(2)}) collective-permute-start(bf16[352,1024]{1,0:T(8,128)(2,1)} %get-tuple-element.19.inner), channel_id=1, source_target_pairs={{0,8},{8,0},{1,9},{9,1},{2,10},{10,2},{3,11},{11,3},{4,12},{12,4},... | collective-permute-start | bytes 2162696 | tf_op jit(solution)/shard_map/ppermute | solution.py:392
  228.7 0.6 collective-permute-start.2
  229.3 2.9 %collective-permute-start = (bf16[352,1024]{1,0:T(8,128)(2,1)}, bf16[352,1024]{1,0:T(8,128)(2,1)S(1)}, u32[]{:S(2)}, u32[]{:S(2)}) collective-permute-start(bf16[352,1024]{1,0:T(8,128)(2,1)} %get-tuple-element.18.inner), channel_id=1, source_target_pairs={{0,8},{8,0},{1,9},{9,1},{2,10},{10,2},{3,11},{11,3},{4,12},{12,4},... | collective-permute-start | bytes 2162696 | tf_op jit(solution)/shard_map/ppermute | solution.py:394
  232.2 0.0 copy-done.3
  232.2 0.6 dynamic_slice.3.flag
  232.8 13.7 %collective-permute-done.1.other = bf16[352,1024]{1,0:T(8,128)(2,1)S(1)} collective-permute-done((bf16[352,1024]{1,0:T(8,128)(2,1)}, bf16[352,1024]{1,0:T(8,128)(2,1)S(1)}, u32[]{:S(2)}, u32[]{:S(2)}) %collective-permute-start.1) | collective-permute-done | bytes 720928 | tf_op jit(solution)/shard_map/ppermute | solution.py:392
  246.5 0.0 copy-start.1
  246.5 0.9 copy-done.1
  247.3 5.3 %outer_step.3 = (bf16[2,352,1024]{2,1,0:T(8,128)(2,1)}, f32[2,352,1024]{2,1,0:T(8,128)}, f32[2,352,1024]{2,1,0:T(8,128)}) custom-call(s32[1]{0:T(128)} %dynamic_slice.3.flag, bf16[352,1024]{1,0:T(8,128)(2,1)} %get-tuple-element.19.inner, bf16[352,1024]{1,0:T(8,128)(2,1)} %copy-done.1, f32[2,352,1024]{2,1,0:T(8,128)} %bitcast.29, f32[2,352,1024]{2,1,0:T(8,128)} %bitcast.31), custom_call_target="tpu_custom_call" | custom-call | flops 3604480 | bytes 7929856 | tf_op jit(solution)/shard_map/outer_step/pallas_call | solution.py:344
  252.7 8.4 %collective-permute-done.2.other = bf16[352,1024]{1,0:T(8,128)(2,1)S(1)} collective-permute-done((bf16[352,1024]{1,0:T(8,128)(2,1)}, bf16[352,1024]{1,0:T(8,128)(2,1)S(1)}, u32[]{:S(2)}, u32[]{:S(2)}) %collective-permute-start.2) | collective-permute-done | bytes 720928 | tf_op jit(solution)/shard_map/ppermute | solution.py:397
  261.1 0.0 copy-start
  261.1 0.9 copy-done
  262.0 5.3 %outer_step.5 = (bf16[1,352,1024]{2,1,0:T(8,128)(2,1)}, f32[1,352,1024]{2,1,0:T(8,128)}, f32[1,352,1024]{2,1,0:T(8,128)}) custom-call(s32[1]{0:T(128)} %dynamic_slice.3.flag, bf16[352,1024]{1,0:T(8,128)(2,1)} %get-tuple-element.24.inner, bf16[352,1024]{1,0:T(8,128)(2,1)} %copy-done, f32[1,352,1024]{2,1,0:T(8,128)} %outer.1, f32[1,352,1024]{2,1,0:T(8,128)} %moment.1), custom_call_target="tpu_custom_call" | custom-call | flops 3604480 | bytes 7929856 | tf_op jit(solution)/shard_map/outer_step/pallas_call | solution.py:344
  267.3 1.5 collective-permute-done.other
  268.8 0.0 copy-start.2
  268.8 0.9 copy-done.2
  269.7 5.3 %outer_step.4 = (bf16[2,352,1024]{2,1,0:T(8,128)(2,1)}, f32[2,352,1024]{2,1,0:T(8,128)}, f32[2,352,1024]{2,1,0:T(8,128)}) custom-call(s32[1]{0:T(128)} %dynamic_slice.3.flag, bf16[352,1024]{1,0:T(8,128)(2,1)} %get-tuple-element.18.inner, bf16[352,1024]{1,0:T(8,128)(2,1)} %copy-done.2, ...), custom_call_target="tpu_custom_call", output_to_operand_aliasing={{0}: (5, {}), {1}: (6, {}), {2}: (7, {})} | custom-call | flops 3604480 | bytes 7929856 | tf_op jit(solution)/shard_map/outer_step/pallas_call | solution.py:344
  (2 shorter events, 0.0 us)
Async XLA Ops:
  0.6 231.6 %copy-start.3 = (s32[8]{0:T(128)S(1)}, s32[8]{0:T(128)}, u32[]{:S(2)}) copy-start(s32[8]{0:T(128)} %param.19) | copy-start | bytes 100
  225.7 20.8 %collective-permute-start.1 = (bf16[352,1024]{1,0:T(8,128)(2,1)}, bf16[352,1024]{1,0:T(8,128)(2,1)S(1)}, u32[]{:S(2)}, u32[]{:S(2)}) collective-permute-start(bf16[352,1024]{1,0:T(8,128)(2,1)} %get-tuple-element.19.inner), channel_id=1, source_target_pairs={{0,8},{8,0},{1,9},{9,1},{2,10},{10,2},{3,11},{11,3},{4,12},{12,4},... | collective-permute-start | bytes 2162696 | tf_op jit(solution)/shard_map/ppermute | solution.py:392
  228.7 32.4 %collective-permute-start.2 = (bf16[352,1024]{1,0:T(8,128)(2,1)}, bf16[352,1024]{1,0:T(8,128)(2,1)S(1)}, u32[]{:S(2)}, u32[]{:S(2)}) collective-permute-start(bf16[352,1024]{1,0:T(8,128)(2,1)} %get-tuple-element.24.inner), channel_id=1, source_target_pairs={{0,8},{8,0},{1,9},{9,1},{2,10},{10,2},{3,11},{11,3},{4,12},{12,4},... | collective-permute-start | bytes 2162696 | tf_op jit(solution)/shard_map/ppermute | solution.py:397
  229.3 39.5 %collective-permute-start = (bf16[352,1024]{1,0:T(8,128)(2,1)}, bf16[352,1024]{1,0:T(8,128)(2,1)S(1)}, u32[]{:S(2)}, u32[]{:S(2)}) collective-permute-start(bf16[352,1024]{1,0:T(8,128)(2,1)} %get-tuple-element.18.inner), channel_id=1, source_target_pairs={{0,8},{8,0},{1,9},{9,1},{2,10},{10,2},{3,11},{11,3},{4,12},{12,4},... | collective-permute-start | bytes 2162696 | tf_op jit(solution)/shard_map/ppermute | solution.py:394
  246.5 0.9 copy-start.1
  261.1 0.9 copy-start
  268.8 0.9 copy-start.2
